TPU v7x, 32 devices: a whole 2x2x4 slice. The times are simulated.
32 devices in a mesh: dp: 8 (over z, y), rep: 4 (over x, core).
Axes of the slice: x: 2, y: 2, z: 4, core: 2. Of those that a mesh axis runs over, the one named last changes fastest.
Arguments:
- tokens: bfloat16 [32768, 768], P(('dp', 'rep')), may hold values from -6 to 6
- qkv_weight: bfloat16 [768, 2304], P('dp'), may hold values from -0.21875 to 0.21875
- out_weight: bfloat16 [768, 768], P('dp'), may hold values from -0.875 to 0.875
- up_weight: bfloat16 [768, 3072], P('dp'), may hold values from -0.21875 to 0.21875
- down_weight: bfloat16 [3072, 768], P('dp'), may hold values from -0.109375 to 0.109375
- norm_gains: bfloat16 [2, 768], P(None, 'dp'), may hold values from 0.5 to 1.5
- bias_rows: bfloat16 [6, 768], P(None, 'dp'), may hold values from -3 to 3
- ff_bias: bfloat16 [3072], P('dp'), may hold values from -3 to 3
- lengths: int32 [288], replicated, may hold values from 32 to 512, as said below
- owners: int32 [288], replicated, may hold values from 0 to 31, as said below
- cotangent: bfloat16 [32768, 768], P(('dp', 'rep')), may hold values from -6 to 6
Outputs:
- output: bfloat16 [32768, 768], P(('dp', 'rep'))
- grad_tokens: float32 [32768, 768], P(('dp', 'rep'))
- grad_qkv: float32 [768, 2304], P('dp')
- grad_out_weight: float32 [768, 768], P('dp')
- grad_up_weight: float32 [768, 3072], P('dp')
- grad_down_weight: float32 [3072, 768], P('dp')
- grad_norm_gains: float32 [2, 768], P(None, 'dp')
- grad_bias_rows: float32 [6, 768], P(None, 'dp')
- grad_ff_bias: float32 [3072], P('dp')
Inputs may be any that keep to these rules, and one draw needn't show every extreme that they name: Passage p holds lengths[p] tokens and belongs to device owners[p]. Every device holds exactly 9 passages, at most one of them longer than 64; a device's passages hold at most 1024 tokens together, and some device's hold exactly 1024. `owners`: each device number appears exactly 9 times.
All inputs are finite; a program needn't handle non-finite values.
Results may differ from a plain program's by a relative error of at most 0.017.
Values may be sent and summed in bfloat16 or wider, within the bound.
A program may use at most 192 MiB of HBM per device.

v0:
```python
import functools

import jax
import jax.numpy as jnp
from jax import lax
from jax.experimental import pallas as pl
from jax.experimental.pallas import tpu as pltpu
from jax.sharding import PartitionSpec as P

HEADS = 12
HD = 64
LONG = 512
SHORT = 64
norm_eps = 1e-06
masked_score = -1000000000.0
BF = jnp.bfloat16
F32 = jnp.float32
VMEM_LIMIT = 62 * 1024 * 1024

NN = (((1,), (0,)), ((), ()))
NT = (((1,), (1,)), ((), ()))
TN = (((0,), (0,)), ((), ()))


def dot(a, b, dims=NN):
    return lax.dot_general(a, b, dims, preferred_element_type=F32)


def vm():
    return pl.BlockSpec(memory_space=pltpu.VMEM)


def sm():
    return pl.BlockSpec(memory_space=pltpu.SMEM)


def params(**kw):
    return pltpu.CompilerParams(vmem_limit_bytes=VMEM_LIMIT, **kw)


def table_kernel(per, me_ref, own_ref, len_ref, tab_ref):
    total = own_ref.shape[0]
    me = me_ref[0]

    def zero(i, c):
        tab_ref[0, i] = 0
        return c

    lax.fori_loop(0, 128, zero, 0)

    def scan(p, c):
        count, start = c
        hit = own_ref[p] == me
        size = len_ref[p]
        tab_ref[0, count] = start
        tab_ref[0, 16 + count] = size
        return (count + hit.astype(jnp.int32), start + jnp.where(hit, size, 0))

    lax.fori_loop(0, total, scan, (jnp.int32(0), jnp.int32(0)), unroll=8)

    def find(j, c):
        return jnp.where(tab_ref[0, 16 + j] > SHORT, j, c)

    big = lax.fori_loop(0, per, find, jnp.int32(0))

    def place(j, slot):
        is_big = j == big
        tab_ref[0, 32 + j] = jnp.where(is_big, 0, LONG + SHORT * slot)
        tab_ref[0, 48 + j] = jnp.where(is_big, LONG // SHORT, 1)
        at = jnp.where(is_big, 0, slot + 1)
        tab_ref[0, 64 + at] = tab_ref[0, 16 + j]
        tab_ref[0, 80 + at] = tab_ref[0, j]
        return slot + jnp.where(is_big, 0, 1)

    lax.fori_loop(0, per, place, jnp.int32(0))


def slot_table(me, owners, lengths, per):
    return pl.pallas_call(
        functools.partial(table_kernel, per),
        out_shape=jax.ShapeDtypeStruct((1, 128), jnp.int32),
        in_specs=[sm(), sm(), sm()],
        out_specs=sm(),
        compiler_params=params(),
        name="table",
    )(me, owners, lengths)


def slot_source(tab_ref, block, shape, dim):
    at = lax.broadcasted_iota(jnp.int32, shape, dim)
    if block == 0:
        return jnp.where(at < tab_ref[0, 64], tab_ref[0, 80] + at, -1)
    source = jnp.full(shape, -1, jnp.int32)
    for s in range(LONG // SHORT):
        inner = at - s * SHORT
        good = (inner >= 0) & (inner < tab_ref[0, 65 + s])
        source = jnp.where(good, tab_ref[0, 81 + s] + inner, source)
    return source


def fill_selection(tab_ref, pick, back):
    for a in range(2):
        for b in range(2):
            slot, row = (b, a) if back else (a, b)
            source = slot_source(tab_ref, slot, (1, LONG) if back else (LONG, 1), 1 if back else 0)
            want = lax.broadcasted_iota(jnp.int32, (LONG, LONG), 0 if back else 1) + row * LONG
            pick[a, b] = jnp.where(source == want, 1.0, 0.0).astype(BF)


def move_rows(pick, srcs, dst):
    for a in range(2):
        total = None
        for b in range(2):
            for src in srcs:
                part = dot(pick[a, b], src[b * LONG : (b + 1) * LONG, :])
                total = part if total is None else total + part
        dst[a * LONG : (a + 1) * LONG, :] = total.astype(dst.dtype)


def permute_kernel(back, tab_ref, src_ref, out_ref, pick):
    fill_selection(tab_ref, pick, back)
    if out_ref.dtype == BF:
        return move_rows(pick, [src_ref], out_ref)
    value = src_ref[...]
    for k in range(3):
        part = value.astype(BF)
        value = value - part.astype(F32)
        for a in range(2):
            at = slice(a * LONG, (a + 1) * LONG)
            old = jnp.zeros((LONG, value.shape[1]), F32) if k == 0 else out_ref[at, :]
            for b in range(2):
                old = old + dot(pick[a, b], part[b * LONG : (b + 1) * LONG, :])
            out_ref[at, :] = old


def permute(tab, src, back):
    return pl.pallas_call(
        functools.partial(permute_kernel, back),
        out_shape=jax.ShapeDtypeStruct(src.shape, src.dtype),
        in_specs=[sm(), vm()],
        out_specs=vm(),
        scratch_shapes=[pltpu.VMEM((2, 2, LONG, LONG), BF)],
        compiler_params=params(),
        name="permute",
    )(tab, src)


def place_of():
    dp, rep = lax.axis_index("dp"), lax.axis_index("rep")
    return dp // 2, dp % 2, rep // 2, rep % 2


def peers(z, y, x, c):
    def at(z2, y2, x2, c2):
        return (z2 * 2 + y2, x2 * 2 + c2)

    return (
        [at((z + k) % 4, y, x, c) for k in (1, 2, 3)],
        at(z, 1 - y, x, c),
        at(z, y, 1 - x, c),
        at(z, y, x, 1 - c),
    )


def greet(zs, yp, xp, cp):
    barrier = pltpu.get_barrier_semaphore()
    for peer in (*zs, yp, xp, cp):
        pl.semaphore_signal(barrier, inc=1, device_id=peer, device_id_type=pl.DeviceIdType.MESH)
    pl.semaphore_wait(barrier, 6)


def remote(src, dst, ssem, rsem, peer):
    return pltpu.make_async_remote_copy(
        src_ref=src, dst_ref=dst, send_sem=ssem, recv_sem=rsem,
        device_id=peer, device_id_type=pl.DeviceIdType.MESH,
    )


def blocks(shard):
    rows, columns = shard.shape
    return shard.reshape(2, 3, rows // 6, columns)


def head_lanes(block, head):
    lane = lax.broadcasted_iota(jnp.int32, (1, block.shape[1]), 1)
    keep = jnp.where(lane >= HD, float(head), 1.0 - head)
    return block * keep.astype(BF)


def softmax_keys(scores, valid):
    scores = jnp.where(valid, scores, masked_score)
    weights = jnp.exp(scores - jnp.max(scores, axis=0, keepdims=True))
    return weights * (1.0 / jnp.sum(weights, axis=0, keepdims=True))


def short_valid(tab_ref, pair, size):
    key = lax.broadcasted_iota(jnp.int32, (size, size), 0)
    query = lax.broadcasted_iota(jnp.int32, (size, size), 1)
    low, high = tab_ref[0, 65 + 2 * pair], tab_ref[0, 66 + 2 * pair]
    bound = jnp.where(key >= SHORT, SHORT + high, low)
    return (key < bound) & (key // SHORT == query // SHORT)


def attend_kernel(scale, tab_ref, q_ref, k_ref, v_ref, out_ref, long_ref, short_ref):
    two = 2 * SHORT
    key = lax.broadcasted_iota(jnp.int32, (LONG, LONG), 0)
    valid = key < tab_ref[0, 64]
    shorts = (q_ref.shape[0] - LONG) // two
    keeps = [short_valid(tab_ref, b, two) for b in range(shorts)]
    total = None
    tails = [None] * shorts
    for h in range(2):
        scores = dot(head_lanes(k_ref[0:LONG], h), q_ref[0:LONG], NT) * scale
        probs = softmax_keys(scores, valid).astype(BF)
        long_ref[h] = probs
        part = dot(probs, head_lanes(v_ref[0:LONG], h), TN)
        total = part if total is None else total + part
        for b in range(shorts):
            rows = slice(LONG + b * two, LONG + (b + 1) * two)
            scores = dot(head_lanes(k_ref[rows], h), q_ref[rows], NT) * scale
            probs = softmax_keys(scores, keeps[b]).astype(BF)
            short_ref[h, b * two : (b + 1) * two] = probs
            part = dot(probs, head_lanes(v_ref[rows], h), TN)
            tails[b] = part if tails[b] is None else tails[b] + part
    out_ref[0:LONG] = total.astype(BF)
    for b in range(shorts):
        out_ref[LONG + b * two : LONG + (b + 1) * two] = tails[b].astype(BF)


def attend(tab, projected):
    rows, wide = projected.shape
    width = wide // 3
    pairs = width // (2 * HD)
    column = lambda off: pl.BlockSpec((rows, 2 * HD), lambda i, off=off: (0, off + i))
    return pl.pallas_call(
        functools.partial(attend_kernel, HD ** (-0.5)),
        grid=(pairs,),
        out_shape=(
            jax.ShapeDtypeStruct((rows, width), BF),
            jax.ShapeDtypeStruct((2 * pairs, LONG, LONG), BF),
            jax.ShapeDtypeStruct((2 * pairs, rows - LONG, 2 * SHORT), BF),
        ),
        in_specs=[sm(), column(0), column(pairs), column(2 * pairs)],
        out_specs=(
            column(0),
            pl.BlockSpec((2, LONG, LONG), lambda i: (i, 0, 0)),
            pl.BlockSpec((2, rows - LONG, 2 * SHORT), lambda i: (i, 0, 0)),
        ),
        compiler_params=params(),
        name="attend",
    )(tab, projected, projected, projected)


def attend_back_kernel(scale, q_ref, k_ref, v_ref, g_ref, long_ref, short_ref, out_ref):
    two = 2 * SHORT
    shorts = (q_ref.shape[0] - LONG) // two
    spans = [(slice(0, LONG), None)]
    spans += [(slice(LONG + b * two, LONG + (b + 1) * two), b) for b in range(shorts)]
    for rows, b in spans:
        sums = None
        for h in range(2):
            probs = long_ref[h] if b is None else short_ref[h, b * two : (b + 1) * two]
            grad = head_lanes(g_ref[rows], h)
            wide = probs.astype(F32)
            grad_probs = dot(v_ref[rows], grad, NT)
            mean = jnp.sum(grad_probs * wide, axis=0, keepdims=True)
            grad_scores = (wide * (grad_probs - mean)).astype(BF)
            parts = (
                dot(grad_scores, head_lanes(k_ref[rows], h), TN),
                dot(grad_scores, head_lanes(q_ref[rows], h)),
                dot(probs, grad),
            )
            sums = parts if sums is None else tuple(a + p for a, p in zip(sums, parts))
        out_ref[0, rows] = (sums[0] * scale).astype(BF)
        out_ref[1, rows] = (sums[1] * scale).astype(BF)
        out_ref[2, rows] = sums[2].astype(BF)


def attend_back(projected, grad_mixed, long_probs, short_probs):
    rows, wide = projected.shape
    width = wide // 3
    pairs = width // (2 * HD)
    column = lambda off: pl.BlockSpec((rows, 2 * HD), lambda i, off=off: (0, off + i))
    return pl.pallas_call(
        functools.partial(attend_back_kernel, HD ** (-0.5)),
        grid=(pairs,),
        out_shape=jax.ShapeDtypeStruct((3, rows, width), BF),
        in_specs=[
            column(0), column(pairs), column(2 * pairs), column(0),
            pl.BlockSpec((2, LONG, LONG), lambda i: (i, 0, 0)),
            pl.BlockSpec((2, rows - LONG, 2 * SHORT), lambda i: (i, 0, 0)),
        ],
        out_specs=pl.BlockSpec((3, rows, 2 * HD), lambda i: (0, 0, i)),
        compiler_params=params(),
        name="attend_back",
    )(projected, projected, projected, grad_mixed, long_probs, short_probs)


def gelu_pair(value):
    size = jnp.abs(value)
    bell = jnp.exp(-0.5 * value * value)
    t = 1.0 / (1.0 + 0.23164189 * size)
    tail = t * (0.127414796 + t * (-0.142248368 + t * (0.7107068705 + t * (-0.7265760135 + t * 0.5307027145))))
    tail = tail * bell
    whole = jnp.where(value >= 0.0, 1.0 - tail, tail)
    return (value * whole, whole + value * bell * 0.3989422804)


def middle_kernel(
    step, span, mixed, tokens, cot, w_out, w_up, w_down, gains, biases, ff_bias,
    out, acc, g_mixed, d_out, d_up, d_down, sums, d_ffb, unit, low, low2, hidden, slope, inv
):
    rows = mixed.shape[0]
    parts = w_up.shape[1] // span
    sums[...] = jnp.zeros_like(sums)

    def rows_at(i):
        return pl.ds(pl.multiple_of(i * step, step), step)

    def columns_at(j):
        return pl.ds(pl.multiple_of(j * span, span), span)

    def mean(a):
        return jnp.mean(a, axis=-1, keepdims=True)

    def tally(i, a):
        sums[i : i + 1, :] += jnp.sum(a, axis=0, keepdims=True)

    def norm(r):
        center = r - mean(r)
        scale = lax.rsqrt(mean(center * center) + norm_eps)
        return center * scale, scale

    def back(s, u, scale):
        return scale * (s - mean(s) - u * mean(s * u))

    @pl.loop(0, rows // step)
    def _(i):
        at = rows_at(i)
        branch = dot(mixed[at, :], w_out[...]) + biases[2:3, :]
        u, scale = norm(tokens[at, :].astype(F32) + branch)
        unit[at, :] = u
        inv[at, :] = scale
        low[at, :] = (u * gains[0:1, :] + biases[4:5, :]).astype(BF)
        acc[at, :] = jnp.zeros((step, acc.shape[1]), F32)

    @pl.loop(0, parts)
    def _(j):
        cols = columns_at(j)
        for i in range(rows // step):
            at = slice(i * step, (i + 1) * step)
            inner = dot(low[at, :], w_up[:, cols]) + ff_bias[:, cols]
            act, der = gelu_pair(inner)
            act = act.astype(BF)
            hidden[at, cols] = act
            slope[at, cols] = der.astype(BF)
            acc[at, :] += dot(act, w_down[cols, :])

    @pl.loop(0, rows // step)
    def _(i):
        at = rows_at(i)
        first = unit[at, :] * gains[0:1, :] + biases[4:5, :]
        u, scale = norm(first + acc[at, :] + biases[3:4, :])
        out[at, :] = (u * gains[1:2, :] + biases[5:6, :]).astype(BF)
        g = cot[at, :].astype(F32)
        tally(1, g * u)
        tally(5, g)
        g = back(g * gains[1:2, :], u, scale)
        acc[at, :] = g
        g = g.astype(BF)
        low2[at, :] = g
        tally(3, g.astype(F32))

    @pl.loop(0, parts)
    def _(j):
        cols = columns_at(j)
        total = None
        for i in range(rows // step):
            at = slice(i * step, (i + 1) * step)
            g = dot(low2[at, :], w_down[cols, :], NT) * slope[at, cols].astype(F32)
            g = g.astype(BF)
            slope[at, cols] = g
            part = jnp.sum(g.astype(F32), axis=0, keepdims=True)
            total = part if total is None else total + part
            acc[at, :] += dot(g, w_up[:, cols], NT)
        d_ffb[:, cols] = total
        d_down[cols, :] = dot(hidden[:, cols], low2[...], TN).astype(BF)
        d_up[:, cols] = dot(low[...], slope[:, cols], TN).astype(BF)

    @pl.loop(0, rows // step)
    def _(i):
        at = rows_at(i)
        g, u = acc[at, :], unit[at, :]
        tally(0, g * u)
        tally(4, g)
        g = back(g * gains[0:1, :], u, inv[at, :])
        acc[at, :] = g
        g = g.astype(BF)
        low2[at, :] = g
        tally(2, g.astype(F32))
        g_mixed[at, :] = dot(g, w_out[...], NT).astype(BF)

    d_out[...] = dot(mixed[...], low2[...], TN).astype(BF)


def middle(mixed, tokens, cot, w_out, w_up, w_down, gains, biases, ff_bias):
    rows, width = mixed.shape
    ff = w_up.shape[1]
    shape = jax.ShapeDtypeStruct
    return pl.pallas_call(
        functools.partial(middle_kernel, 256, 512),
        out_shape=(
            shape((rows, width), BF), shape((rows, width), F32), shape((rows, width), BF),
            shape((width, width), BF), shape((width, ff), BF), shape((ff, width), BF),
            shape((8, width), F32), shape((1, ff), F32),
        ),
        in_specs=[vm()] * 9,
        out_specs=(vm(),) * 8,
        scratch_shapes=[
            pltpu.VMEM((rows, width), F32), pltpu.VMEM((rows, width), BF),
            pltpu.VMEM((rows, width), BF), pltpu.VMEM((rows, ff), BF),
            pltpu.VMEM((rows, ff), BF), pltpu.VMEM((rows, 1), F32),
        ],
        compiler_params=params(),
        name="middle",
    )(mixed, tokens, cot, w_out, w_up, w_down, gains, biases, ff_bias)


def head_kernel(scale, pairs, tab, *refs):
    n = 5
    shards, raw, raw_cot = refs[:n], refs[n], refs[n + 1]
    fulls = refs[n + 2 : 2 * n + 2]
    projected, mixed, long_hbm, short_hbm, tokens, cot = refs[2 * n + 2 : 2 * n + 8]
    ssem, rsem, lsem, osem, bias, long_buf, short_buf = refs[2 * n + 8 :]
    z, y, x, c = place_of()
    zs, yp, xp, cp = peers(z, y, x, c)
    greet(zs, yp, xp, cp)
    width = tokens.shape[1]
    two = 2 * HD
    sent = []

    def go(w, i, src, dst, peer):
        copy = remote(src, dst, ssem.at[w, i], rsem.at[w, i], peer)
        copy.start()
        sent.append(copy)

    def arrive(w, i, ref):
        remote(ref, ref, ssem.at[w, i], rsem.at[w, i], cp).wait_recv()

    def local(w):
        return pltpu.make_async_copy(shards[w], fulls[w].at[z, y], lsem.at[w])

    def near(w):
        local(w).start()
        src = shards[w].at[c, pl.ds(x, 2)]
        dst = fulls[w].at[z, y, c, pl.ds(x, 2)]
        for k in range(3):
            go(w, k, src, dst, zs[k])
        go(w, 3, src, dst, yp)

    def mid_at(w, k):
        zk = (z + 3 - k) % 4
        part = fulls[w].at[zk, y, c, pl.ds(x, 2)]
        arrive(w, k, part)
        go(w, 4 + k, part, part, yp)
        q = fulls[w].at[zk, y, c, 2 * x]
        go(w, 7 + k, q, q, xp)

    def far_at(w, k):
        zk = (z + 4 - k) % 4
        part = fulls[w].at[zk, 1 - y, c, pl.ds(x, 2)]
        arrive(w, 3 + k, part)
        q = fulls[w].at[zk, 1 - y, c, 2 * x]
        go(w, 10 + k, q, q, xp)

    def mid(w):
        for k in range(3):
            mid_at(w, k)

    def far(w):
        for k in range(4):
            far_at(w, k)

    def across(w):
        for k in range(7):
            zk, yk = ((z + 3 - k) % 4, y) if k < 3 else ((z + 7 - k) % 4, 1 - y)
            arrive(w, 7 + k, fulls[w].at[zk, yk, c, 2 * (1 - x)])
            part = fulls[w].at[zk, yk, c]
            go(w, 14 + k, part, part, cp)

    def last(w):
        for k in range(7):
            zk, yk = ((z + 3 - k) % 4, y) if k < 3 else ((z + 7 - k) % 4, 1 - y)
            arrive(w, 14 + k, fulls[w].at[zk, yk, 1 - c])
        local(w).wait()

    def project():
        cut = width // 8
        rows = [fulls[0][i // 2, i % 2, 0, 0].astype(F32) for i in range(8)]
        bias[...] = jnp.zeros_like(bias)
        bias[:, 0:width] = jnp.concatenate([r[0:1, 0:cut] for r in rows], 1)
        bias[:, 2 * width :] = jnp.concatenate([r[1:2, 0:cut] for r in rows], 1)
        span = width // 2

        @pl.loop(0, 6)
        def _(j):
            cols = pl.ds(pl.multiple_of(j * span, span), span)
            part = fulls[1][:, :, :, :, :, cols].reshape(width, span)
            projected[:, cols] = (dot(tokens[...], part) + bias[:, cols]).astype(BF)

    def store(i):
        return (
            pltpu.make_async_copy(long_buf.at[i % 2], long_hbm.at[2 * i : 2 * i + 2], osem.at[i % 2]),
            pltpu.make_async_copy(short_buf.at[i % 2], short_hbm.at[2 * i : 2 * i + 2], osem.at[2 + i % 2]),
        )

    def attend_at(i):
        if i >= 2:
            for copy in store(i - 2):
                copy.wait()
        at = pl.ds(i * two, two)
        attend_kernel(
            scale, tab,
            projected.at[:, at],
            projected.at[:, pl.ds(width + i * two, two)],
            projected.at[:, pl.ds(2 * width + i * two, two)],
            mixed.at[:, at], long_buf.at[i % 2], short_buf.at[i % 2],
        )
        for copy in store(i):
            copy.start()

    for w in range(n):
        near(w)
    fill_selection(tab, long_buf, False)
    move_rows(long_buf, [raw], tokens)
    move_rows(long_buf, [raw_cot], cot)
    mid(0)
    mid(1)
    far(0)
    far(1)
    across(0)
    across(1)
    mid(2)
    last(0)
    last(1)
    far(2)
    project()
    across(2)
    attend_at(0)
    mid_at(3, 0)
    attend_at(1)
    mid_at(3, 1)
    attend_at(2)
    far_at(3, 0)
    mid_at(3, 2)
    attend_at(3)
    far_at(3, 1)
    attend_at(4)
    far_at(3, 2)
    mid_at(4, 0)
    attend_at(5)
    far_at(3, 3)
    last(2)
    mid_at(4, 1)
    far_at(4, 0)
    across(3)
    mid_at(4, 2)
    far_at(4, 1)
    far_at(4, 2)
    far_at(4, 3)
    last(3)
    across(4)
    last(4)
    for i in (pairs - 2, pairs - 1):
        for copy in store(i):
            copy.wait()
    for copy in sent:
        copy.wait_send()


def head(tab, shards, tokens, cotangent):
    n = len(shards)
    views = [blocks(s) for s in shards]
    rows, width = tokens.shape
    pairs = width // (2 * HD)
    shape = jax.ShapeDtypeStruct
    anywhere = pl.BlockSpec(memory_space=pl.ANY)
    results = pl.pallas_call(
        functools.partial(head_kernel, HD ** (-0.5), pairs),
        out_shape=[shape((4, 2) + v.shape, v.dtype) for v in views]
        + [
            shape((rows, 3 * width), BF), shape((rows, width), BF),
            shape((2 * pairs, LONG, LONG), BF), shape((2 * pairs, rows - LONG, 2 * SHORT), BF),
            shape((rows, width), BF), shape((rows, width), BF),
        ],
        in_specs=[sm()] + [vm()] * (n + 2),
        out_specs=[vm()] * 2 + [anywhere] * 3 + [vm()] * 2 + [anywhere] * 2 + [vm()] * 2,
        scratch_shapes=[
            pltpu.SemaphoreType.DMA((n, 21)), pltpu.SemaphoreType.DMA((n, 21)),
            pltpu.SemaphoreType.DMA((n,)), pltpu.SemaphoreType.DMA((4,)),
            pltpu.VMEM((1, 3 * width), F32),
            pltpu.VMEM((2, 2, LONG, LONG), BF), pltpu.VMEM((2, 2, rows - LONG, 2 * SHORT), BF),
        ],
        compiler_params=params(collective_id=0, has_side_effects=True),
        name="head",
    )(tab, *views, tokens, cotangent)
    return [f.reshape(8 * s.shape[0], s.shape[1]) for f, s in zip(results, shards)], results[n:]


def tail_kernel(scale, pairs, tab, *refs):
    d_down, d_up, d_out, small_in, projected, g_mixed, tokens, grad_one, long_hbm, short_hbm, w_hbm = refs[:11]
    outs, grad_tokens = refs[11:16], refs[16]
    own = refs[17:]
    n = 5
    half, rx, rpy, rqy, rpz, rqz, rpx, fin, got = (own[i * n : (i + 1) * n] for i in range(9))
    ssem, rsem, lsem, d_qkv, small, heads, long_buf, short_buf, w_qkv = own[9 * n :]
    grads = [d_down, d_up, d_out, d_qkv, small]
    z, y, x, c = place_of()
    zs, yp, xp, cp = peers(z, y, x, c)
    width = tokens.shape[1]
    two = 2 * HD
    sent = []

    def fetch(i):
        return (
            pltpu.make_async_copy(long_hbm.at[2 * i : 2 * i + 2], long_buf.at[i % 2], lsem.at[i % 2]),
            pltpu.make_async_copy(short_hbm.at[2 * i : 2 * i + 2], short_buf.at[i % 2], lsem.at[2 + i % 2]),
        )

    weights = pltpu.make_async_copy(w_hbm, w_qkv, lsem.at[4])
    weights.start()
    for copy in fetch(0):
        copy.start()
    small[...] = small_in[...]
    greet(zs, yp, xp, cp)

    def go(w, i, src, dst, peer):
        copy = remote(src, dst, ssem.at[w, i], rsem.at[w, i], peer)
        copy.start()
        sent.append(copy)

    def arrive(w, i, ref):
        remote(ref, ref, ssem.at[w, i], rsem.at[w, i], cp).wait_recv()

    def add(*parts):
        total = parts[0].astype(F32)
        for part in parts[1:]:
            total = total + part.astype(F32)
        return total

    def s0(w):
        go(w, 0, grads[w].at[:, :, 1 - c], half[w], cp)

    def s1(w):
        arrive(w, 0, half[w])
        a = half[w]

        @pl.loop(0, 4)
        def _(i):
            for j in range(2):
                for k in range(3):
                    a[i, j, k] = add(grads[w][i, j, c, k], a[i, j, k]).astype(a.dtype)

        go(w, 1, a.at[:, :, 2 * (1 - x)], rx[w], xp)
        go(w, 2, a.at[:, 1 - y, 1], rpy[w], yp)

    def s2p(w):
        a = half[w]
        arrive(w, 2, rpy[w])

        @pl.loop(0, 4)
        def _(i):
            a[i, y, 1] = add(a[i, y, 1], rpy[w][i]).astype(a.dtype)

        for k in range(3):
            go(w, 3 + k, a.at[(z + k + 1) % 4, y, 1], rpz[w].at[k], zs[k])

    def s2q(w):
        a = half[w]
        arrive(w, 1, rx[w])

        @pl.loop(0, 4)
        def _(i):
            for j in range(2):
                a[i, j, 2 * x] = add(a[i, j, 2 * x], rx[w][i, j]).astype(a.dtype)

        go(w, 6, a.at[:, 1 - y, 2 * x], rqy[w], yp)

    def s3p(w):
        a = half[w]
        for k in range(3):
            arrive(w, 3 + k, rpz[w].at[k])
        a[z, y, 1] = add(a[z, y, 1], rpz[w][0], rpz[w][1], rpz[w][2]).astype(a.dtype)
        go(w, 10, a.at[z, y, 1], rpx[w], xp)

    def s3q(w):
        a = half[w]
        arrive(w, 6, rqy[w])

        @pl.loop(0, 4)
        def _(i):
            a[i, y, 2 * x] = add(a[i, y, 2 * x], rqy[w][i]).astype(a.dtype)

        for k in range(3):
            go(w, 7 + k, a.at[(z + k + 1) % 4, y, 2 * x], rqz[w].at[k], zs[k])

    def s4p(w):
        a = half[w]
        arrive(w, 10, rpx[w])
        fin[w][1] = add(a[z, y, 1], rpx[w][...]).astype(a.dtype)
        go(w, 14, fin[w].at[1], got[w].at[c, 1], cp)

    def s4q(w):
        a = half[w]
        for k in range(3):
            arrive(w, 7 + k, rqz[w].at[k])
        fin[w][0] = add(a[z, y, 2 * x], rqz[w][0], rqz[w][1], rqz[w][2]).astype(a.dtype)
        go(w, 11, fin[w].at[0], got[w].at[c, 2 * x], xp)
        go(w, 13, fin[w].at[0], got[w].at[c, 2 * x], cp)

    def s5(w):
        arrive(w, 11, got[w].at[c, 2 * (1 - x)])
        piece = got[w].at[c, 2 * (1 - x)]
        go(w, 12, piece, piece, cp)
        outs[w][c, 2 * x] = fin[w][0].astype(F32)
        outs[w][c, 1] = fin[w][1].astype(F32)
        outs[w][c, 2 * (1 - x)] = got[w][c, 2 * (1 - x)].astype(F32)

    def s6(w):
        arrive(w, 12, got[w].at[1 - c, 2 * (1 - x)])
        arrive(w, 13, got[w].at[1 - c, 2 * x])
        arrive(w, 14, got[w].at[1 - c, 1])
        for k in range(3):
            outs[w][1 - c, k] = got[w][1 - c, k].astype(F32)

    def back(i):
        if i + 1 < pairs:
            for copy in fetch(i + 1):
                copy.start()
        for copy in fetch(i):
            copy.wait()
        at = pl.ds(i * two, two)
        attend_back_kernel(
            scale,
            projected.at[:, at],
            projected.at[:, pl.ds(width + i * two, two)],
            projected.at[:, pl.ds(2 * width + i * two, two)],
            g_mixed.at[:, at],
            long_buf.at[i % 2], short_buf.at[i % 2],
            heads.at[:, :, at],
        )

    def weight(k):
        part = 256
        for j in range(width // part):
            at = slice(j * part, (j + 1) * part)
            value = dot(tokens[...], heads[k, :, at], TN).astype(BF)
            d_qkv[:, :, :, :, :, k * width + j * part : k * width + (j + 1) * part] = value.reshape(
                d_qkv.shape[:5] + (part,)
            )
        if k != 1:
            total = jnp.sum(heads[k].astype(F32), axis=0, keepdims=True)
            cut = width // 8
            for i in range(8):
                row = k // 2
                small[i // 2, i % 2, 0, 0, row : row + 1, 0:cut] = total[:, i * cut : (i + 1) * cut]

    def rows_back(i):
        step = tokens.shape[0] // 4
        at = slice(i * step, (i + 1) * step)
        total = grad_one[at, :]
        for k in range(3):
            total = total + dot(heads[k, at, :], w_qkv[:, k * width : (k + 1) * width], NT)
        for k in range(3):
            part = total.astype(BF)
            total = total - part.astype(F32)
            heads[k, at, :] = part

    def select(_):
        fill_selection(tab, long_buf, True)

    def token_rows(_):
        move_rows(long_buf, [heads.at[0], heads.at[1], heads.at[2]], grad_tokens)

    def run(*steps):
        for f, *which in steps:
            for w in which:
                f(w)

    run(
        (s0, 0, 1, 2), (back, 0, 1), (s1, 0), (back, 2), (s1, 1), (back, 3, 4), (s2p, 0), (back, 5),
        (s2p, 1), (weight, 0), (s2q, 0), (weight, 1, 2), (s0, 3, 4), (s3p, 0), (s3q, 0), (select, 0),
    )
    weights.wait()
    run(
        (rows_back, 0), (s1, 3, 2, 4), (s3p, 1), (s4q, 0), (s4p, 0), (rows_back, 1), (s2q, 1),
        (s2p, 3, 2, 4), (rows_back, 2), (s3q, 1), (s4p, 1), (s5, 0), (rows_back, 3), (token_rows, 0), (s2q, 3),
        (s3p, 3, 2, 4), (s4q, 1), (s2q, 2, 4), (s3q, 3), (s5, 1), (s3q, 2, 4), (s4p, 3, 2, 4),
        (s6, 0), (s4q, 3), (s6, 1), (s4q, 2, 4), (s5, 3, 2, 4), (s6, 3, 2, 4),
    )
    for copy in sent:
        copy.wait_send()


def tail(tab, d_down, d_up, d_out, small, projected, g_mixed, tokens, grad_one, long_probs, short_probs, w_qkv):
    rows, wide = projected.shape
    width = wide // 3
    pairs = width // (2 * HD)

    def view(shape):
        return (4, 2, 2, 3, shape[0] // 48, shape[1])

    views = [g.reshape(view(g.shape)) for g in (d_down, d_up, d_out)] + [small.reshape(view(small.shape))]
    qkv_view = view(w_qkv.shape)
    kinds = [(v.shape, v.dtype) for v in views[:3]] + [(qkv_view, BF), (views[3].shape, F32)]
    lead = ((4, 2, 3), (4, 2), (4,), (4,), (3,), (3,), (), (2,), (2, 3))
    scratch = [pltpu.VMEM(s + v[4:], t) for s in lead for v, t in kinds]
    anywhere = pl.BlockSpec(memory_space=pl.ANY)
    results = pl.pallas_call(
        functools.partial(tail_kernel, HD ** (-0.5), pairs),
        out_shape=[jax.ShapeDtypeStruct(v[2:], F32) for v, _ in kinds]
        + [jax.ShapeDtypeStruct((rows, width), F32)],
        in_specs=[sm()] + [vm()] * 8 + [anywhere] * 3,
        out_specs=[vm()] * 6,
        scratch_shapes=scratch
        + [
            pltpu.SemaphoreType.DMA((5, 15)), pltpu.SemaphoreType.DMA((5, 15)),
            pltpu.SemaphoreType.DMA((5,)),
            pltpu.VMEM(qkv_view, BF), pltpu.VMEM(views[3].shape, F32),
            pltpu.VMEM((3, rows, width), BF),
            pltpu.VMEM((2, 2) + long_probs.shape[1:], BF),
            pltpu.VMEM((2, 2) + short_probs.shape[1:], BF),
            pltpu.VMEM(w_qkv.shape, BF),
        ],
        compiler_params=params(collective_id=1, has_side_effects=True),
        name="tail",
    )(tab, *views, projected, g_mixed, tokens, grad_one, long_probs, short_probs, w_qkv)
    flat = [o.reshape(-1, o.shape[-1]) for o in results[:5]]
    return flat, results[5]


def square():
    return lax.axis_size("dp") == 8 and lax.axis_size("rep") == 4


def front_layer(tab, tokens, cotangent, qkv_weight, out_weight, up_weight, down_weight, norm_gains, bias_rows, ff_bias):
    width = tokens.shape[1]
    if not square():
        tokens, cotangent = permute(tab, tokens, False), permute(tab, cotangent, False)
        w_qkv, w_out, w_up, w_down = (
            lax.all_gather(w, "dp", axis=0, tiled=True)
            for w in (qkv_weight, out_weight, up_weight, down_weight)
        )
        gains = lax.all_gather(norm_gains, "dp", axis=1, tiled=True)
        biases = lax.all_gather(bias_rows, "dp", axis=1, tiled=True)
        up_bias = lax.all_gather(ff_bias, "dp", axis=0, tiled=True)
        wide = biases.astype(F32)
        bias = jnp.concatenate([wide[0], jnp.zeros((width,), F32), wide[1]])
        projected = (dot(tokens, w_qkv) + bias).astype(BF)
        mixed, *probs = attend(tab, projected)
        return (
            w_qkv, w_out, w_up, w_down, gains, biases, up_bias,
            tokens, cotangent, projected, mixed, tuple(probs),
        )

    cut = width // 8
    kept = bias_rows.shape[0] - 2
    rest = jnp.concatenate([bias_rows[2:].reshape(-1), norm_gains.reshape(-1), ff_bias])
    used = rest.shape[0]
    first = jnp.pad(bias_rows[:2], ((0, 14), (0, 128 - cut)))
    rest = jnp.pad(rest, (0, 80 * 128 - used)).reshape(80, 128)
    small = jnp.concatenate([first, rest])
    full, (projected, mixed, *probs, tokens, cotangent) = head(
        tab, [small, qkv_weight, out_weight, up_weight, down_weight], tokens, cotangent
    )
    rows = full[0].reshape(8, 96, 128)
    lead = rows[:, :2, :cut]
    rows = rows[:, 16:].reshape(8, -1)[:, :used]
    nb, ng = kept * cut, norm_gains.shape[0] * cut
    biases = jnp.concatenate([lead, rows[:, :nb].reshape(8, kept, cut)], 1).transpose(1, 0, 2)
    gains = rows[:, nb : nb + ng].reshape(8, -1, cut).transpose(1, 0, 2)
    return (
        full[1], full[2], full[3], full[4],
        gains.reshape(-1, width), biases.reshape(-1, width), rows[:, nb + ng :].reshape(-1),
        tokens, cotangent, projected, mixed, tuple(probs),
    )


def reduce_layer(d_qkv, d_out, d_up, d_down, d_gains, d_biases, d_up_bias):
    def full(g):
        part = lax.psum_scatter(g, "rep", scatter_dimension=1, tiled=True).astype(F32)
        part = lax.psum_scatter(part, "dp", scatter_dimension=0, tiled=True)
        return lax.all_gather(part.astype(BF), "rep", axis=1, tiled=True).astype(F32)

    small = lax.psum(
        (
            lax.psum_scatter(d_gains, "dp", scatter_dimension=1, tiled=True),
            lax.psum_scatter(d_biases, "dp", scatter_dimension=1, tiled=True),
            lax.psum_scatter(d_up_bias, "dp", scatter_dimension=0, tiled=True),
        ),
        "rep",
    )
    return tuple(full(g.astype(BF)) for g in (d_qkv, d_out, d_up, d_down)) + small


def back_layer(tab, final, projected, grad_mixed, probs, tokens, grad_one, w_qkv, d_out, d_up, d_down, sums, d_up_bias):
    width = tokens.shape[1]
    if not square():
        parts = attend_back(projected, grad_mixed, *probs)
        grad_heads = jnp.concatenate([parts[0], parts[1], parts[2]], 1)
        d_head = jnp.sum(grad_heads.astype(F32), axis=0)[None]
        d_qkv = dot(tokens, grad_heads, TN)
        grad_tokens = grad_one + dot(grad_heads, w_qkv, NT)
        d_biases = jnp.concatenate([d_head[:, :width], d_head[:, 2 * width :], sums[2:6]])
        moved = (permute(tab, final, True), permute(tab, grad_tokens, True))
        return moved + reduce_layer(d_qkv, d_out, d_up, d_down, sums[0:2], d_biases, d_up_bias)

    def cut(g):
        return g.reshape(g.shape[0], 8, -1).transpose(1, 0, 2).reshape(8, -1)

    rest = jnp.concatenate([cut(sums[0:6]), d_up_bias.reshape(8, -1)], 1)
    n0, n1 = 6 * (width // 8), rest.shape[1]
    small = jnp.pad(rest, ((0, 0), (1024, 5 * 1024 - n1))).reshape(8 * 48, 128)
    (down, up, out, qkv, own), grad_tokens = tail(
        tab, d_down, d_up, d_out, small, projected, grad_mixed, tokens, grad_one, *probs, w_qkv
    )
    own_rest = own[8:].reshape(-1)
    rows = own_rest[:n0].reshape(6, -1)
    biases = jnp.concatenate([own[0:2, : width // 8], rows[2:6]])
    return (permute(tab, final, True), grad_tokens, qkv, out, up, down, rows[0:2], biases, own_rest[n0:n1])


def local(
    tokens,
    qkv_weight,
    out_weight,
    up_weight,
    down_weight,
    norm_gains,
    bias_rows,
    ff_bias,
    lengths,
    owners,
    cotangent,
):
    row_count = tokens.shape[0]
    device = lax.axis_index("dp") * lax.axis_size("rep") + lax.axis_index("rep")
    devices = lax.axis_size("dp") * lax.axis_size("rep")
    per = lengths.shape[0] // devices
    assert row_count == LONG + SHORT * (per - 1) == 2 * LONG
    me = device.astype(jnp.int32).reshape(1)
    tab = slot_table(me, owners, lengths, per)
    w_qkv, w_out, w_up, w_down, gains, biases, up_bias, tokens, cotangent, projected, mixed_rows, probs = front_layer(
        tab, tokens, cotangent, qkv_weight, out_weight, up_weight, down_weight, norm_gains, bias_rows, ff_bias
    )
    gain_rows = gains.astype(F32)
    shift_rows = biases.astype(F32)
    up_bias = up_bias.astype(F32)
    final, grad_one, grad_mixed, d_out, d_up, d_down, sums, d_up_bias = middle(
        mixed_rows, tokens, cotangent, w_out, w_up, w_down, gain_rows, shift_rows, up_bias[None]
    )
    d_up_bias = d_up_bias[0]
    return back_layer(
        tab, final, projected, grad_mixed, probs, tokens, grad_one, w_qkv,
        d_out, d_up, d_down, sums, d_up_bias,
    )


def solution(mesh):
    in_specs = (
        P(("dp", "rep"), None),
        P("dp", None),
        P("dp", None),
        P("dp", None),
        P("dp", None),
        P(None, "dp"),
        P(None, "dp"),
        P("dp"),
        P(),
        P(),
        P(("dp", "rep"), None),
    )
    out_specs = (
        P(("dp", "rep"), None),
        P(("dp", "rep"), None),
        P("dp", None),
        P("dp", None),
        P("dp", None),
        P("dp", None),
        P(None, "dp"),
        P(None, "dp"),
        P("dp"),
    )
    return jax.shard_map(local, mesh=mesh, in_specs=in_specs, out_specs=out_specs, check_vma=False)
```

profile of v0, /device:TPU:0, one launch (start us, length us, event | category | flops | bytes accessed | tf_op | source)
XLA Modules:
  0.0 294.8 jit_solution(13865435456389562798)
XLA Ops:
  0.6 3.4 %table.1.tab.tab_ref = s32[1,128]{1,0:T(1,128)} custom-call(s32[1]{0:T(128)} %bitcast.me_ref, s32[288]{0:T(512)} %own_ref.1, s32[288]{0:T(512)} %len_ref.1), custom_call_target="tpu_custom_call" | custom-call | tf_op jit(solution)/shard_map/table/pallas_call | solution.py:79
  4.1 0.7 slice.57
  4.8 0.1 reshape.126
  4.8 0.7 reshape.127
  5.6 0.8 fusion.9
  6.3 0.7 slice.56
  7.0 0.6 fusion.6
  7.6 87.8 %head.1 = (bf16[4,2,2,3,16,128]{5,4,3,2,1,0:T(8,128)(2,1)}, bf16[4,2,2,3,16,2304]{5,4,3,2,1,0:T(8,128)(2,1)}, bf16[4,2,2,3,16,768]{5,4,3,2,1,0:T(8,128)(2,1)}, b...) custom-call(s32[1,128]{1,0:T(1,128)} %table.1.tab.tab_ref, ...), custom_call_target="tpu_custom_call" | custom-call | tf_op jit(solution)/shard_map/head/pallas_call | solution.py:588
  95.4 0.9 slice_bitcast_fusion
  96.4 0.1 convert_bitcast_fusion.1
  96.5 0.1 reshape.138
  96.6 0.7 slice.73
  97.3 0.7 reshape.152.biases
  98.0 0.6 copy.30
  98.6 0.1 reshape.154
  98.7 0.7 reshape.151.gains
  99.4 63.3 %middle.1 = (bf16[1024,768]{1,0:T(8,128)(2,1)}, f32[1024,768]{1,0:T(8,128)}, bf16[1024,768]{1,0:T(8,128)(2,1)}, bf16[768,768]{1,0:T(8,128)(2,1)}, bf16[768,3072]...) custom-call(bf16[1024,768]{1,0:T(8,128)(2,1)} %get-tuple-element.34.mixed, ...), custom_call_target="tpu_custom_call" | custom-call | tf_op jit(solution)/shard_map/middle/pallas_call | solution.py:410
  162.6 0.8 reshape.142
  163.5 0.1 reshape.143
  163.5 0.5 broadcast.30
  164.1 1.4 reduce.3
  165.5 0.1 fusion
  165.5 0.7 copy.31
  166.2 112.8 %tail.1 = (f32[2,3,64,768]{3,2,1,0:T(8,128)}, f32[2,3,16,3072]{3,2,1,0:T(8,128)}, f32[2,3,16,768]{3,2,1,0:T(8,128)}, f32[2,3,16,2304]{3,2,1,0:T(8,128)}, f32[2,3,8,128]{3,2,1,0:T(8,128)}, /*index=5*/f32[1024,768]{1,0:T(8,128)}) custom-call(s32[1,128]{1,0:T(1,128)} %table.1.tab.tab_ref, bf16[4,2,2,3,64,768]{5,4,3,2,1,0:T(8,128)(2,1)} %bitcast.46, ...), custom_call_target="tpu_custom_call" | custom-call | tf_op jit(solution)/shard_map/tail/pallas_call | solution.py:819
  279.1 0.7 slice_bitcast_fusion.1
  279.8 0.7 fusion.10
  280.4 0.1 slice.69
  280.5 0.7 slice.78
  281.2 0.6 pad_maximum_fusion
  281.8 0.6 slice.66
  282.4 4.4 %permute.1 = bf16[1024,768]{1,0:T(8,128)(2,1)} custom-call(s32[1,128]{1,0:T(1,128)} %table.1.tab.tab_ref, bf16[1024,768]{1,0:T(8,128)(2,1)} %get-tuple-element.41.src_ref), custom_call_target="tpu_custom_call" | custom-call | tf_op jit(solution)/shard_map/permute/pallas_call | solution.py:137
  286.8 0.0 copy-start.2
  286.8 3.8 %copy.43 = f32[1024,768]{1,0:T(8,128)} copy(f32[1024,768]{1,0:T(8,128)} %get-tuple-element.73) | data formatting | bytes 6291456
  290.6 0.0 copy-done.2
  290.6 0.0 copy-start.3
  290.6 0.0 copy-start.1
  290.7 0.9 copy.44
  291.6 0.2 copy-done.3
  291.8 0.0 copy-start
  291.8 0.7 copy.45
  292.5 0.0 copy-done.1
  292.5 1.0 copy.46
  293.5 0.0 copy-done
  293.5 1.0 copy.47
  (9 shorter events, 0.1 us)
Async XLA Ops:
  286.8 3.8 %copy-start.2 = (f32[2,3,16,2304]{3,2,1,0:T(8,128)S(1)}, f32[2,3,16,2304]{3,2,1,0:T(8,128)}, u32[]{:S(2)}) copy-start(f32[2,3,16,2304]{3,2,1,0:T(8,128)} %get-tuple-element.54) | copy-start | bytes 2654212
  290.6 1.1 copy-start.3
  290.6 1.8 copy-start.1
  291.8 1.7 copy-start
where the time goes:
time: 299 us; the launch traced here: 295 us
  Pallas kernels  272 us (91%)
  local copies, waits for them, and re-layouts  18.7 us (6%)
  other arithmetic  3.52 us (1%)
    pallas_call x1, Pallas kernels, tail(): pl.pallas_call(functools.partial(tail_kernel, HD ** (-0.5), pairs), out_s...  113 us
    pallas_call x1, Pallas kernels, head(): pl.pallas_call(functools.partial(head_kernel, HD ** (-0.5), pairs), out_s...  87.8 us
    pallas_call x1, Pallas kernels, middle(): pl.pallas_call(functools.partial(middle_kernel, 256, 512), out_shape=(sha...  63.3 us
    unnamed x18, local copies, waits for them, and re-layouts  10 us

commit v1 on v0

--- a/solution.py
+++ b/solution.py
@@ -307,7 +307,7 @@
 
 
 def middle_kernel(
-    step, span, mixed, tokens, cot, w_out, w_up, w_down, gains, biases, ff_bias,
+    step, span, mixed, tokens, cot, w_out, w_up, w_down, vectors, ff_bias,
     out, acc, g_mixed, d_out, d_up, d_down, sums, d_ffb, unit, low, low2, hidden, slope, inv
 ):
     rows = mixed.shape[0]
@@ -337,11 +337,11 @@
     @pl.loop(0, rows // step)
     def _(i):
         at = rows_at(i)
-        branch = dot(mixed[at, :], w_out[...]) + biases[2:3, :]
+        branch = dot(mixed[at, :], w_out[...]) + vectors[2:3, :]
         u, scale = norm(tokens[at, :].astype(F32) + branch)
         unit[at, :] = u
         inv[at, :] = scale
-        low[at, :] = (u * gains[0:1, :] + biases[4:5, :]).astype(BF)
+        low[at, :] = (u * vectors[6:7, :] + vectors[4:5, :]).astype(BF)
         acc[at, :] = jnp.zeros((step, acc.shape[1]), F32)
 
     @pl.loop(0, parts)
@@ -359,13 +359,13 @@
     @pl.loop(0, rows // step)
     def _(i):
         at = rows_at(i)
-        first = unit[at, :] * gains[0:1, :] + biases[4:5, :]
-        u, scale = norm(first + acc[at, :] + biases[3:4, :])
-        out[at, :] = (u * gains[1:2, :] + biases[5:6, :]).astype(BF)
+        first = unit[at, :] * vectors[6:7, :] + vectors[4:5, :]
+        u, scale = norm(first + acc[at, :] + vectors[3:4, :])
+        out[at, :] = (u * vectors[7:8, :] + vectors[5:6, :]).astype(BF)
         g = cot[at, :].astype(F32)
         tally(1, g * u)
         tally(5, g)
-        g = back(g * gains[1:2, :], u, scale)
+        g = back(g * vectors[7:8, :], u, scale)
         acc[at, :] = g
         g = g.astype(BF)
         low2[at, :] = g
@@ -393,7 +393,7 @@
         g, u = acc[at, :], unit[at, :]
         tally(0, g * u)
         tally(4, g)
-        g = back(g * gains[0:1, :], u, inv[at, :])
+        g = back(g * vectors[6:7, :], u, inv[at, :])
         acc[at, :] = g
         g = g.astype(BF)
         low2[at, :] = g
@@ -403,7 +403,7 @@
     d_out[...] = dot(mixed[...], low2[...], TN).astype(BF)
 
 
-def middle(mixed, tokens, cot, w_out, w_up, w_down, gains, biases, ff_bias):
+def middle(mixed, tokens, cot, w_out, w_up, w_down, vectors, ff_bias):
     rows, width = mixed.shape
     ff = w_up.shape[1]
     shape = jax.ShapeDtypeStruct
@@ -414,7 +414,7 @@
             shape((width, width), BF), shape((width, ff), BF), shape((ff, width), BF),
             shape((8, width), F32), shape((1, ff), F32),
         ),
-        in_specs=[vm()] * 9,
+        in_specs=[vm()] * 8,
         out_specs=(vm(),) * 8,
         scratch_shapes=[
             pltpu.VMEM((rows, width), F32), pltpu.VMEM((rows, width), BF),
@@ -423,15 +423,27 @@
         ],
         compiler_params=params(),
         name="middle",
-    )(mixed, tokens, cot, w_out, w_up, w_down, gains, biases, ff_bias)
+    )(mixed, tokens, cot, w_out, w_up, w_down, vectors, ff_bias)
 
 
 def head_kernel(scale, pairs, tab, *refs):
     n = 5
-    shards, raw, raw_cot = refs[:n], refs[n], refs[n + 1]
-    fulls = refs[n + 2 : 2 * n + 2]
-    projected, mixed, long_hbm, short_hbm, tokens, cot = refs[2 * n + 2 : 2 * n + 8]
-    ssem, rsem, lsem, osem, bias, long_buf, short_buf = refs[2 * n + 8 :]
+    bias_rows, norm_gains, ff_bias, raw, raw_cot = refs[:5]
+    shards = (None,) + refs[5 : n + 4]
+    fulls = (None,) + refs[n + 4 : 2 * n + 3]
+    projected, mixed, long_hbm, short_hbm, tokens, cot, vectors, wide_bias = refs[2 * n + 3 : 2 * n + 11]
+    ssem, rsem, lsem, osem, bias, long_buf, short_buf, tile, small, small_full = refs[2 * n + 11 :]
+    shards = (small,) + shards[1:]
+    fulls = (small_full,) + fulls[1:]
+    kept, cut = bias_rows.shape
+    tile[...] = jnp.zeros_like(tile)
+    tile[0:kept, 0:cut] = bias_rows[...].astype(F32)
+    tile[kept : kept + 2, 0:cut] = norm_gains[...].astype(F32)
+    pieces = ff_bias.shape[1] // 128
+    for j in range(pieces):
+        tile[8 + j : 9 + j, :] = ff_bias[:, j * 128 : (j + 1) * 128].astype(F32)
+    small[...] = jnp.zeros_like(small)
+    small[0, 0] = tile[...].astype(BF)
     z, y, x, c = place_of()
     zs, yp, xp, cp = peers(z, y, x, c)
     greet(zs, yp, xp, cp)
@@ -495,11 +507,12 @@
         local(w).wait()
 
     def project():
-        cut = width // 8
         rows = [fulls[0][i // 2, i % 2, 0, 0].astype(F32) for i in range(8)]
+        vectors[...] = jnp.concatenate([r[0:8, 0:cut] for r in rows], 1)
+        wide_bias[...] = jnp.concatenate([r[8 + j : 9 + j, :] for r in rows for j in range(pieces)], 1)
         bias[...] = jnp.zeros_like(bias)
-        bias[:, 0:width] = jnp.concatenate([r[0:1, 0:cut] for r in rows], 1)
-        bias[:, 2 * width :] = jnp.concatenate([r[1:2, 0:cut] for r in rows], 1)
+        bias[:, 0:width] = vectors[0:1, :]
+        bias[:, 2 * width :] = vectors[1:2, :]
         span = width // 2
 
         @pl.loop(0, 6)
@@ -578,8 +591,8 @@
         copy.wait_send()
 
 
-def head(tab, shards, tokens, cotangent):
-    n = len(shards)
+def head(tab, bias_rows, norm_gains, ff_bias, shards, tokens, cotangent):
+    n = len(shards) + 1
     views = [blocks(s) for s in shards]
     rows, width = tokens.shape
     pairs = width // (2 * HD)
@@ -592,25 +605,28 @@
             shape((rows, 3 * width), BF), shape((rows, width), BF),
             shape((2 * pairs, LONG, LONG), BF), shape((2 * pairs, rows - LONG, 2 * SHORT), BF),
             shape((rows, width), BF), shape((rows, width), BF),
+            shape((8, width), F32), shape((1, 8 * ff_bias.shape[0]), F32),
         ],
-        in_specs=[sm()] + [vm()] * (n + 2),
-        out_specs=[vm()] * 2 + [anywhere] * 3 + [vm()] * 2 + [anywhere] * 2 + [vm()] * 2,
+        in_specs=[sm()] + [vm()] * (n + 4),
+        out_specs=[vm()] + [anywhere] * 3 + [vm()] * 2 + [anywhere] * 2 + [vm()] * 4,
         scratch_shapes=[
             pltpu.SemaphoreType.DMA((n, 21)), pltpu.SemaphoreType.DMA((n, 21)),
             pltpu.SemaphoreType.DMA((n,)), pltpu.SemaphoreType.DMA((4,)),
             pltpu.VMEM((1, 3 * width), F32),
             pltpu.VMEM((2, 2, LONG, LONG), BF), pltpu.VMEM((2, 2, rows - LONG, 2 * SHORT), BF),
+            pltpu.VMEM((16, 128), F32), pltpu.VMEM((2, 3, 16, 128), BF),
+            pltpu.VMEM((4, 2, 2, 3, 16, 128), BF),
         ],
         compiler_params=params(collective_id=0, has_side_effects=True),
         name="head",
-    )(tab, *views, tokens, cotangent)
-    return [f.reshape(8 * s.shape[0], s.shape[1]) for f, s in zip(results, shards)], results[n:]
+    )(tab, bias_rows, norm_gains, ff_bias[None], tokens, cotangent, *views)
+    return [f.reshape(8 * s.shape[0], s.shape[1]) for f, s in zip(results, shards)], results[n - 1 :]
 
 
 def tail_kernel(scale, pairs, tab, *refs):
-    d_down, d_up, d_out, small_in, projected, g_mixed, tokens, grad_one, long_hbm, short_hbm, w_hbm = refs[:11]
-    outs, grad_tokens = refs[11:16], refs[16]
-    own = refs[17:]
+    d_down, d_up, d_out, sums, d_ffb, projected, g_mixed, tokens, grad_one, long_hbm, short_hbm, w_hbm = refs[:12]
+    outs, grad_tokens = refs[12:17], refs[17]
+    own = refs[18:]
     n = 5
     half, rx, rpy, rqy, rpz, rqz, rpx, fin, got = (own[i * n : (i + 1) * n] for i in range(9))
     ssem, rsem, lsem, d_qkv, small, heads, long_buf, short_buf, w_qkv = own[9 * n :]
@@ -631,7 +647,15 @@
     weights.start()
     for copy in fetch(0):
         copy.start()
-    small[...] = small_in[...]
+    small[...] = jnp.zeros_like(small)
+    cut, long_cut = sums.shape[1] // 8, d_ffb.shape[1] // 8
+    for i in range(8):
+        at = slice(i * cut, (i + 1) * cut)
+        small[i // 2, i % 2, 0, 0, 2:6, 0:cut] = sums[2:6, at]
+        small[i // 2, i % 2, 0, 0, 6:8, 0:cut] = sums[0:2, at]
+        for j in range(long_cut // 128):
+            first = i * long_cut + j * 128
+            small[i // 2, i % 2, 0, 1, j : j + 1, :] = d_ffb[:, first : first + 128]
     greet(zs, yp, xp, cp)
 
     def go(w, i, src, dst, peer):
@@ -760,7 +784,6 @@
             )
         if k != 1:
             total = jnp.sum(heads[k].astype(F32), axis=0, keepdims=True)
-            cut = width // 8
             for i in range(8):
                 row = k // 2
                 small[i // 2, i % 2, 0, 0, row : row + 1, 0:cut] = total[:, i * cut : (i + 1) * cut]
@@ -802,7 +825,7 @@
         copy.wait_send()
 
 
-def tail(tab, d_down, d_up, d_out, small, projected, g_mixed, tokens, grad_one, long_probs, short_probs, w_qkv):
+def tail(tab, d_down, d_up, d_out, sums, d_ffb, projected, g_mixed, tokens, grad_one, long_probs, short_probs, w_qkv):
     rows, wide = projected.shape
     width = wide // 3
     pairs = width // (2 * HD)
@@ -810,9 +833,10 @@
     def view(shape):
         return (4, 2, 2, 3, shape[0] // 48, shape[1])
 
-    views = [g.reshape(view(g.shape)) for g in (d_down, d_up, d_out)] + [small.reshape(view(small.shape))]
+    views = [g.reshape(view(g.shape)) for g in (d_down, d_up, d_out)]
+    small_view = (4, 2, 2, 3, 8, 128)
     qkv_view = view(w_qkv.shape)
-    kinds = [(v.shape, v.dtype) for v in views[:3]] + [(qkv_view, BF), (views[3].shape, F32)]
+    kinds = [(v.shape, v.dtype) for v in views[:3]] + [(qkv_view, BF), (small_view, F32)]
     lead = ((4, 2, 3), (4, 2), (4,), (4,), (3,), (3,), (), (2,), (2, 3))
     scratch = [pltpu.VMEM(s + v[4:], t) for s in lead for v, t in kinds]
     anywhere = pl.BlockSpec(memory_space=pl.ANY)
@@ -820,13 +844,13 @@
         functools.partial(tail_kernel, HD ** (-0.5), pairs),
         out_shape=[jax.ShapeDtypeStruct(v[2:], F32) for v, _ in kinds]
         + [jax.ShapeDtypeStruct((rows, width), F32)],
-        in_specs=[sm()] + [vm()] * 8 + [anywhere] * 3,
+        in_specs=[sm()] + [vm()] * 9 + [anywhere] * 3,
         out_specs=[vm()] * 6,
         scratch_shapes=scratch
         + [
             pltpu.SemaphoreType.DMA((5, 15)), pltpu.SemaphoreType.DMA((5, 15)),
             pltpu.SemaphoreType.DMA((5,)),
-            pltpu.VMEM(qkv_view, BF), pltpu.VMEM(views[3].shape, F32),
+            pltpu.VMEM(qkv_view, BF), pltpu.VMEM(small_view, F32),
             pltpu.VMEM((3, rows, width), BF),
             pltpu.VMEM((2, 2) + long_probs.shape[1:], BF),
             pltpu.VMEM((2, 2) + short_probs.shape[1:], BF),
@@ -834,7 +858,7 @@
         ],
         compiler_params=params(collective_id=1, has_side_effects=True),
         name="tail",
-    )(tab, *views, projected, g_mixed, tokens, grad_one, long_probs, short_probs, w_qkv)
+    )(tab, *views, sums, d_ffb, projected, g_mixed, tokens, grad_one, long_probs, short_probs, w_qkv)
     flat = [o.reshape(-1, o.shape[-1]) for o in results[:5]]
     return flat, results[5]
 
@@ -859,31 +883,15 @@
         projected = (dot(tokens, w_qkv) + bias).astype(BF)
         mixed, *probs = attend(tab, projected)
         return (
-            w_qkv, w_out, w_up, w_down, gains, biases, up_bias,
+            w_qkv, w_out, w_up, w_down,
+            jnp.concatenate([biases, gains]).astype(F32), up_bias.astype(F32)[None],
             tokens, cotangent, projected, mixed, tuple(probs),
         )
 
-    cut = width // 8
-    kept = bias_rows.shape[0] - 2
-    rest = jnp.concatenate([bias_rows[2:].reshape(-1), norm_gains.reshape(-1), ff_bias])
-    used = rest.shape[0]
-    first = jnp.pad(bias_rows[:2], ((0, 14), (0, 128 - cut)))
-    rest = jnp.pad(rest, (0, 80 * 128 - used)).reshape(80, 128)
-    small = jnp.concatenate([first, rest])
-    full, (projected, mixed, *probs, tokens, cotangent) = head(
-        tab, [small, qkv_weight, out_weight, up_weight, down_weight], tokens, cotangent
-    )
-    rows = full[0].reshape(8, 96, 128)
-    lead = rows[:, :2, :cut]
-    rows = rows[:, 16:].reshape(8, -1)[:, :used]
-    nb, ng = kept * cut, norm_gains.shape[0] * cut
-    biases = jnp.concatenate([lead, rows[:, :nb].reshape(8, kept, cut)], 1).transpose(1, 0, 2)
-    gains = rows[:, nb : nb + ng].reshape(8, -1, cut).transpose(1, 0, 2)
-    return (
-        full[1], full[2], full[3], full[4],
-        gains.reshape(-1, width), biases.reshape(-1, width), rows[:, nb + ng :].reshape(-1),
-        tokens, cotangent, projected, mixed, tuple(probs),
-    )
+    full, (projected, mixed, *probs, tokens, cotangent, vectors, up_bias) = head(
+        tab, bias_rows, norm_gains, ff_bias, [qkv_weight, out_weight, up_weight, down_weight], tokens, cotangent
+    )
+    return (*full, vectors, up_bias, tokens, cotangent, projected, mixed, tuple(probs))
 
 
 def reduce_layer(d_qkv, d_out, d_up, d_down, d_gains, d_biases, d_up_bias):
@@ -913,21 +921,16 @@
         grad_tokens = grad_one + dot(grad_heads, w_qkv, NT)
         d_biases = jnp.concatenate([d_head[:, :width], d_head[:, 2 * width :], sums[2:6]])
         moved = (permute(tab, final, True), permute(tab, grad_tokens, True))
-        return moved + reduce_layer(d_qkv, d_out, d_up, d_down, sums[0:2], d_biases, d_up_bias)
-
-    def cut(g):
-        return g.reshape(g.shape[0], 8, -1).transpose(1, 0, 2).reshape(8, -1)
-
-    rest = jnp.concatenate([cut(sums[0:6]), d_up_bias.reshape(8, -1)], 1)
-    n0, n1 = 6 * (width // 8), rest.shape[1]
-    small = jnp.pad(rest, ((0, 0), (1024, 5 * 1024 - n1))).reshape(8 * 48, 128)
+        return moved + reduce_layer(d_qkv, d_out, d_up, d_down, sums[0:2], d_biases, d_up_bias[0])
+
     (down, up, out, qkv, own), grad_tokens = tail(
-        tab, d_down, d_up, d_out, small, projected, grad_mixed, tokens, grad_one, *probs, w_qkv
-    )
-    own_rest = own[8:].reshape(-1)
-    rows = own_rest[:n0].reshape(6, -1)
-    biases = jnp.concatenate([own[0:2, : width // 8], rows[2:6]])
-    return (permute(tab, final, True), grad_tokens, qkv, out, up, down, rows[0:2], biases, own_rest[n0:n1])
+        tab, d_down, d_up, d_out, sums, d_up_bias, projected, grad_mixed, tokens, grad_one, *probs, w_qkv
+    )
+    cut, pieces = width // 8, d_up_bias.shape[1] // (8 * 128)
+    return (
+        permute(tab, final, True), grad_tokens, qkv, out, up, down,
+        own[6:8, :cut], own[0:6, :cut], own[8 : 8 + pieces].reshape(-1),
+    )
 
 
 def local(
@@ -950,16 +953,12 @@
     assert row_count == LONG + SHORT * (per - 1) == 2 * LONG
     me = device.astype(jnp.int32).reshape(1)
     tab = slot_table(me, owners, lengths, per)
-    w_qkv, w_out, w_up, w_down, gains, biases, up_bias, tokens, cotangent, projected, mixed_rows, probs = front_layer(
+    w_qkv, w_out, w_up, w_down, vectors, up_bias, tokens, cotangent, projected, mixed_rows, probs = front_layer(
         tab, tokens, cotangent, qkv_weight, out_weight, up_weight, down_weight, norm_gains, bias_rows, ff_bias
     )
-    gain_rows = gains.astype(F32)
-    shift_rows = biases.astype(F32)
-    up_bias = up_bias.astype(F32)
     final, grad_one, grad_mixed, d_out, d_up, d_down, sums, d_up_bias = middle(
-        mixed_rows, tokens, cotangent, w_out, w_up, w_down, gain_rows, shift_rows, up_bias[None]
-    )
-    d_up_bias = d_up_bias[0]
+        mixed_rows, tokens, cotangent, w_out, w_up, w_down, vectors, up_bias
+    )
     return back_layer(
         tab, final, projected, grad_mixed, probs, tokens, grad_one, w_qkv,
         d_out, d_up, d_down, sums, d_up_bias,

time: 299 us -> 289 us (0.967)
  local copies, waits for them, and re-layouts: 18.7 us -> 12.7 us
  other arithmetic: 3.52 us -> 0 us
    unnamed x18 -> x13, local copies, waits for them, and re-layouts: 10 us -> 7.71 us
where the time goes in v1:
time: 289 us; the launch traced here: 285 us
  Pallas kernels  271 us (94%)
  local copies, waits for them, and re-layouts  12.7 us (4%)
    pallas_call x1, Pallas kernels, tail(): pl.pallas_call(functools.partial(tail_kernel, HD ** (-0.5), pairs), out_s...  113 us
    pallas_call x1, Pallas kernels, head(): pl.pallas_call(functools.partial(head_kernel, HD ** (-0.5), pairs), out_s...  87.6 us
    pallas_call x1, Pallas kernels, middle(): pl.pallas_call(functools.partial(middle_kernel, 256, 512), out_shape=(sha...  63.1 us
    unnamed x13, local copies, waits for them, and re-layouts  7.71 us

profile of v1, /device:TPU:0, one launch (start us, length us, event | category | flops | bytes accessed | tf_op | source)
XLA Modules:
  0.0 284.9 jit_solution(17294410696790981257)
XLA Ops:
  0.6 3.4 %table.1.tab.tab_ref = s32[1,128]{1,0:T(1,128)} custom-call(s32[1]{0:T(128)} %bitcast.me_ref, s32[288]{0:T(512)} %own_ref.1, s32[288]{0:T(512)} %len_ref.1), custom_call_target="tpu_custom_call" | custom-call | tf_op jit(solution)/shard_map/table/pallas_call | solution.py:79
  4.1 1.2 broadcast_in_dim.3.refs_2_
  5.3 87.6 %head.1 = (bf16[4,2,2,3,16,2304]{5,4,3,2,1,0:T(8,128)(2,1)}, bf16[4,2,2,3,16,768]{5,4,3,2,1,0:T(8,128)(2,1)}, bf16[4,2,2,3,16,3072]{5,4,3,2,1,0:T(8,128)(2,1)}, ...) custom-call(s32[1,128]{1,0:T(1,128)} %table.1.tab.tab_ref, ...), custom_call_target="tpu_custom_call" | custom-call | tf_op jit(solution)/shard_map/head/pallas_call | solution.py:601
  92.9 63.1 %middle.1 = (bf16[1024,768]{1,0:T(8,128)(2,1)}, f32[1024,768]{1,0:T(8,128)}, bf16[1024,768]{1,0:T(8,128)(2,1)}, bf16[768,768]{1,0:T(8,128)(2,1)}, bf16[768,3072]...) custom-call(bf16[1024,768]{1,0:T(8,128)(2,1)} %get-tuple-element.35.mixed, ...), custom_call_target="tpu_custom_call" | custom-call | tf_op jit(solution)/shard_map/middle/pallas_call | solution.py:410
  156.0 4.4 %permute.1 = bf16[1024,768]{1,0:T(8,128)(2,1)} custom-call(s32[1,128]{1,0:T(1,128)} %table.1.tab.tab_ref, bf16[1024,768]{1,0:T(8,128)(2,1)} %get-tuple-element.43.src_ref), custom_call_target="tpu_custom_call" | custom-call | tf_op jit(solution)/shard_map/permute/pallas_call | solution.py:137
  160.3 112.8 %tail.1 = (f32[2,3,64,768]{3,2,1,0:T(8,128)}, f32[2,3,16,3072]{3,2,1,0:T(8,128)}, f32[2,3,16,768]{3,2,1,0:T(8,128)}, f32[2,3,16,2304]{3,2,1,0:T(8,128)}, f32[2,3,8,128]{3,2,1,0:T(8,128)}, /*index=5*/f32[1024,768]{1,0:T(8,128)}) custom-call(s32[1,128]{1,0:T(1,128)} %table.1.tab.tab_ref, bf16[4,2,2,3,64,768]{5,4,3,2,1,0:T(8,128)(2,1)} %bitcast.20, ...), custom_call_target="tpu_custom_call" | custom-call | tf_op jit(solution)/shard_map/tail/pallas_call | solution.py:843
  273.2 1.2 slice.12
  274.4 1.3 slice_bitcast_fusion
  275.6 1.3 slice.13
  276.9 0.0 copy-start.2
  276.9 3.8 %copy.25 = f32[1024,768]{1,0:T(8,128)} copy(f32[1024,768]{1,0:T(8,128)} %get-tuple-element.71) | data formatting | bytes 6291456
  280.7 0.0 copy-done.2
  280.8 0.0 copy-start.3
  280.8 0.0 copy-start.1
  280.8 0.9 copy.26
  281.7 0.2 copy-done.3
  281.9 0.0 copy-start
  281.9 0.7 copy.27
  282.6 0.0 copy-done.1
  282.6 1.0 copy.28
  283.6 0.0 copy-done
  283.6 1.0 copy.29
Async XLA Ops:
  276.9 3.8 %copy-start.2 = (f32[2,3,16,2304]{3,2,1,0:T(8,128)S(1)}, f32[2,3,16,2304]{3,2,1,0:T(8,128)}, u32[]{:S(2)}) copy-start(f32[2,3,16,2304]{3,2,1,0:T(8,128)} %get-tuple-element.56) | copy-start | bytes 2654212
  280.8 1.1 copy-start.3
  280.8 1.8 copy-start.1
  281.9 1.7 copy-start

commit v2 on v1

--- a/solution.py
+++ b/solution.py
@@ -542,7 +542,7 @@
         for copy in store(i):
             copy.start()
 
-    for w in range(n):
+    for w in (0, 1, 3, 4, 2):
         near(w)
     fill_selection(tab, long_buf, False)
     move_rows(long_buf, [raw], tokens)
@@ -553,37 +553,37 @@
     far(1)
     across(0)
     across(1)
-    mid(2)
     last(0)
     last(1)
-    far(2)
     project()
-    across(2)
+    mid_at(3, 0)
     attend_at(0)
-    mid_at(3, 0)
+    mid_at(3, 1)
+    mid_at(3, 2)
     attend_at(1)
-    mid_at(3, 1)
+    far_at(3, 0)
     attend_at(2)
-    far_at(3, 0)
-    mid_at(3, 2)
+    far_at(3, 1)
     attend_at(3)
-    far_at(3, 1)
+    mid_at(4, 0)
+    far_at(3, 2)
     attend_at(4)
-    far_at(3, 2)
-    mid_at(4, 0)
+    mid_at(4, 1)
+    far_at(3, 3)
     attend_at(5)
-    far_at(3, 3)
-    last(2)
-    mid_at(4, 1)
     far_at(4, 0)
+    mid_at(4, 2)
     across(3)
-    mid_at(4, 2)
     far_at(4, 1)
+    mid(2)
     far_at(4, 2)
     far_at(4, 3)
+    far(2)
     last(3)
     across(4)
+    across(2)
     last(4)
+    last(2)
     for i in (pairs - 2, pairs - 1):
         for copy in store(i):
             copy.wait()

time: 289 us -> 287 us (level)
  no operation moved by 1% of the time
where the time goes in v2:
time: 287 us; the launch traced here: 283 us
  Pallas kernels  269 us (94%)
  local copies, waits for them, and re-layouts  12.7 us (4%)
    pallas_call x1, Pallas kernels, tail(): pl.pallas_call(functools.partial(tail_kernel, HD ** (-0.5), pairs), out_s...  112 us
    pallas_call x1, Pallas kernels, head(): pl.pallas_call(functools.partial(head_kernel, HD ** (-0.5), pairs), out_s...  87 us
    pallas_call x1, Pallas kernels, middle(): pl.pallas_call(functools.partial(middle_kernel, 256, 512), out_shape=(sha...  63.1 us
    unnamed x13, local copies, waits for them, and re-layouts  7.71 us

profile of v2, /device:TPU:0, one launch (start us, length us, event | category | flops | bytes accessed | tf_op | source)
XLA Modules:
  0.0 283.0 jit_solution(16219631221339627245)
XLA Ops:
  0.6 3.4 %table.1.tab.tab_ref = s32[1,128]{1,0:T(1,128)} custom-call(s32[1]{0:T(128)} %bitcast.me_ref, s32[288]{0:T(512)} %own_ref.1, s32[288]{0:T(512)} %len_ref.1), custom_call_target="tpu_custom_call" | custom-call | tf_op jit(solution)/shard_map/table/pallas_call | solution.py:79
  4.1 1.2 broadcast_in_dim.3.refs_2_
  5.3 87.0 %head.1 = (bf16[4,2,2,3,16,2304]{5,4,3,2,1,0:T(8,128)(2,1)}, bf16[4,2,2,3,16,768]{5,4,3,2,1,0:T(8,128)(2,1)}, bf16[4,2,2,3,16,3072]{5,4,3,2,1,0:T(8,128)(2,1)}, ...) custom-call(s32[1,128]{1,0:T(1,128)} %table.1.tab.tab_ref, ...), custom_call_target="tpu_custom_call" | custom-call | tf_op jit(solution)/shard_map/head/pallas_call | solution.py:601
  92.3 63.1 %middle.1 = (bf16[1024,768]{1,0:T(8,128)(2,1)}, f32[1024,768]{1,0:T(8,128)}, bf16[1024,768]{1,0:T(8,128)(2,1)}, bf16[768,768]{1,0:T(8,128)(2,1)}, bf16[768,3072]...) custom-call(bf16[1024,768]{1,0:T(8,128)(2,1)} %get-tuple-element.35.mixed, ...), custom_call_target="tpu_custom_call" | custom-call | tf_op jit(solution)/shard_map/middle/pallas_call | solution.py:410
  155.4 4.4 %permute.1 = bf16[1024,768]{1,0:T(8,128)(2,1)} custom-call(s32[1,128]{1,0:T(1,128)} %table.1.tab.tab_ref, bf16[1024,768]{1,0:T(8,128)(2,1)} %get-tuple-element.43.src_ref), custom_call_target="tpu_custom_call" | custom-call | tf_op jit(solution)/shard_map/permute/pallas_call | solution.py:137
  159.7 111.6 %tail.1 = (f32[2,3,64,768]{3,2,1,0:T(8,128)}, f32[2,3,16,3072]{3,2,1,0:T(8,128)}, f32[2,3,16,768]{3,2,1,0:T(8,128)}, f32[2,3,16,2304]{3,2,1,0:T(8,128)}, f32[2,3,8,128]{3,2,1,0:T(8,128)}, /*index=5*/f32[1024,768]{1,0:T(8,128)}) custom-call(s32[1,128]{1,0:T(1,128)} %table.1.tab.tab_ref, bf16[4,2,2,3,64,768]{5,4,3,2,1,0:T(8,128)(2,1)} %bitcast.20, ...), custom_call_target="tpu_custom_call" | custom-call | tf_op jit(solution)/shard_map/tail/pallas_call | solution.py:843
  271.3 1.2 slice.12
  272.5 1.3 slice_bitcast_fusion
  273.8 1.3 slice.13
  275.0 0.0 copy-start.2
  275.0 3.8 %copy.25 = f32[1024,768]{1,0:T(8,128)} copy(f32[1024,768]{1,0:T(8,128)} %get-tuple-element.71) | data formatting | bytes 6291456
  278.9 0.0 copy-done.2
  278.9 0.0 copy-start.3
  278.9 0.0 copy-start.1
  278.9 0.9 copy.26
  279.8 0.2 copy-done.3
  280.0 0.0 copy-start
  280.0 0.7 copy.27
  280.7 0.0 copy-done.1
  280.7 1.0 copy.28
  281.7 0.0 copy-done
  281.7 1.0 copy.29
Async XLA Ops:
  275.0 3.8 %copy-start.2 = (f32[2,3,16,2304]{3,2,1,0:T(8,128)S(1)}, f32[2,3,16,2304]{3,2,1,0:T(8,128)}, u32[]{:S(2)}) copy-start(f32[2,3,16,2304]{3,2,1,0:T(8,128)} %get-tuple-element.56) | copy-start | bytes 2654212
  278.9 1.1 copy-start.3
  278.9 1.8 copy-start.1
  280.0 1.7 copy-start
